TPU v7x, 32 devices: a whole 2x2x4 slice. The times are simulated.
32 devices in a mesh: row: 8 (over z, x), col: 2 (over core), dp: 2 (over y).
Axes of the slice: x: 2, y: 2, z: 4, core: 2. Of those that a mesh axis runs over, the one named last changes fastest.
Arguments:
- pixels: bfloat16 [2, 3, 256, 256], P('dp', None, 'row', 'col'), may hold values from -6 to 6
- cotangent: bfloat16 [2, 64, 64, 1024], P('dp', 'row', 'col'), may hold values from -6 to 6
- embed_weight: bfloat16 [48, 1024], replicated, may hold values from -0.875 to 0.875
- embed_bias: float32 [1024], replicated, may hold values from -4 to 4
- layer_norm_gain: float32 [1024], replicated, may hold values from 0.5 to 1.5
- qkv_weight: bfloat16 [1024, 2304], P('row', ('col', 'dp')), may hold values from -0.1875 to 0.1875
- out_weight: bfloat16 [768, 1024], P('row', ('col', 'dp')), may hold values from -0.21875 to 0.21875
- bias_table: float32 [12, 225], replicated, may hold values from -4 to 404
- rel_index: int32 [64, 64], replicated, may hold values from 0 to 224
- shifts: int32 [2, 2], P('dp'), may hold values from 1 to 7
Outputs:
- out_weight_grad: float32 [768, 1024], P('row', ('col', 'dp'))
- embed_weight_grad: float32 [48, 1024], replicated
- embed_bias_grad: float32 [1024], replicated
- norm_gain_grad: float32 [1024], replicated
- bias_table_grad: float32 [12, 225], replicated
Inputs may be any that keep to these rules, and one draw needn't show every extreme that they name: `rel_index`: each entry names one of the 225 columns of bias_table.
All inputs are finite; a program needn't handle non-finite values.
Results may differ from a plain program's by a relative error of at most 0.023.
Values may be sent and summed in bfloat16 or wider, within the bound.
A program may use at most 64 MiB of HBM per device.

v0:
```python
import jax
import jax.numpy as jnp
from jax import lax
from jax.sharding import PartitionSpec as P

WIN = 8
PATCH = 4
norm_epsilon = 1e-05


def from_behind(value, axis, steps):
    count = lax.axis_size(axis)
    pairs = [(source, (source + steps) % count) for source in range(count)]
    return lax.ppermute(value, axis, pairs)


def make_patches(pixel_block):
    images, channels, pixel_rows, pixel_cols = pixel_block.shape
    grid_rows = pixel_rows // PATCH
    grid_cols = pixel_cols // PATCH
    shaped = pixel_block.reshape(images, channels, grid_rows, PATCH, grid_cols, PATCH)
    return shaped.transpose(0, 2, 4, 1, 3, 5).reshape(
        images, grid_rows, grid_cols, channels * PATCH * PATCH
    )


def embed_cells(patches, embed_weight, embed_bias):
    return (jnp.dot(patches, embed_weight, preferred_element_type=jnp.float32) + embed_bias).astype(
        jnp.bfloat16
    )


def window_split(block):
    rows_all, cols_all, features = block.shape
    shaped = block.reshape(rows_all // WIN, WIN, cols_all // WIN, WIN, features)
    return shaped.transpose(0, 2, 1, 3, 4).reshape(-1, WIN * WIN, features)


def window_join(windows, rows_all, cols_all):
    features = windows.shape[-1]
    shaped = windows.reshape(rows_all // WIN, cols_all // WIN, WIN, WIN, features)
    return shaped.transpose(0, 2, 1, 3, 4).reshape(rows_all, cols_all, features)


def splice_after(own_block, borrowed, offsets, along_dim):
    length = own_block.shape[along_dim]

    def single(own_item, borrowed_item, offset):
        joined = jnp.concatenate([own_item, borrowed_item], along_dim - 1)
        return lax.dynamic_slice_in_dim(joined, offset, length, along_dim - 1)

    return jax.vmap(single)(own_block, borrowed, offsets)


def splice_before(own_block, borrowed, offsets, along_dim):
    length = own_block.shape[along_dim]
    margin = borrowed.shape[along_dim]

    def single(own_item, borrowed_item, offset):
        joined = jnp.concatenate([borrowed_item, own_item], along_dim - 1)
        return lax.dynamic_slice_in_dim(joined, margin - offset, length, along_dim - 1)

    return jax.vmap(single)(own_block, borrowed, offsets)


def attend_forward(cell_windows, labels, layer_norm_gain, qkv_full, bias_full):
    window_count, cell_count, features = cell_windows.shape
    head_count = bias_full.shape[0]
    inner_width = qkv_full.shape[1] // 3
    head_size = inner_width // head_count
    score_scale = head_size ** (-0.5)
    flat_rows = cell_windows.reshape(-1, features).astype(jnp.float32)
    average = jnp.mean(flat_rows, axis=-1, keepdims=True)
    centered_input = flat_rows - average
    inverse_deviation = lax.rsqrt(
        jnp.mean(centered_input * centered_input, axis=-1, keepdims=True) + norm_epsilon
    )
    standardized_rows = centered_input * inverse_deviation
    normalized_rows = (standardized_rows * layer_norm_gain).astype(jnp.bfloat16)
    projected = jnp.dot(normalized_rows, qkv_full, preferred_element_type=jnp.float32).astype(
        jnp.bfloat16
    )
    head_shape = (window_count, cell_count, head_count, head_size)
    query_rows = projected[:, :inner_width].reshape(head_shape)
    key_vectors = projected[:, inner_width : 2 * inner_width].reshape(head_shape)
    value_rows = projected[:, 2 * inner_width :].reshape(head_shape)
    scores = (
        jnp.einsum("wmhd,wnhd->whmn", query_rows, key_vectors, preferred_element_type=jnp.float32)
        * score_scale
        + bias_full[None]
    )
    same_region = labels[:, None, :, None] == labels[:, None, None, :]
    scores = jnp.where(same_region, scores, -1e30)
    row_peak = jnp.max(scores, axis=-1, keepdims=True)
    exp_scores = jnp.exp(scores - row_peak)
    attention_weights = exp_scores / jnp.sum(exp_scores, axis=-1, keepdims=True)
    reduced_probability = attention_weights.astype(jnp.bfloat16)
    attended = jnp.einsum(
        "whmn,wnhd->wmhd", reduced_probability, value_rows, preferred_element_type=jnp.float32
    ).astype(jnp.bfloat16)
    stored_residuals = (
        standardized_rows,
        inverse_deviation,
        query_rows,
        key_vectors,
        value_rows,
        attention_weights,
        reduced_probability,
    )
    return (stored_residuals, attended.reshape(-1, inner_width))


def attend_backward(stored_residuals, d_attended, layer_norm_gain, qkv_full):
    (
        standardized_rows,
        inverse_deviation,
        query_rows,
        key_vectors,
        value_rows,
        attention_weights,
        reduced_probability,
    ) = stored_residuals
    head_shape = query_rows.shape
    score_scale = head_shape[3] ** (-0.5)
    total_row_count = standardized_rows.shape[0]
    inner_width = head_shape[2] * head_shape[3]
    d_heads = d_attended.reshape(head_shape)
    d_prob = jnp.einsum("wmhd,wnhd->whmn", d_heads, value_rows, preferred_element_type=jnp.float32)
    d_values = jnp.einsum(
        "whmn,wmhd->wnhd", reduced_probability, d_heads, preferred_element_type=jnp.float32
    ).astype(jnp.bfloat16)
    d_scores = attention_weights * (
        d_prob - jnp.sum(attention_weights * d_prob, axis=-1, keepdims=True)
    )
    table_part = jnp.sum(d_scores, axis=0)
    d_low = d_scores.astype(jnp.bfloat16)
    d_queries = (
        jnp.einsum("whmn,wnhd->wmhd", d_low, key_vectors, preferred_element_type=jnp.float32)
        * score_scale
    ).astype(jnp.bfloat16)
    d_keys = (
        jnp.einsum("whmn,wmhd->wnhd", d_low, query_rows, preferred_element_type=jnp.float32)
        * score_scale
    ).astype(jnp.bfloat16)
    d_projected = jnp.concatenate(
        [
            d_queries.reshape(total_row_count, inner_width),
            d_keys.reshape(total_row_count, inner_width),
            d_values.reshape(total_row_count, inner_width),
        ],
        axis=1,
    )
    normalized_gradient = lax.dot_general(
        d_projected, qkv_full, (((1,), (1,)), ((), ())), preferred_element_type=jnp.float32
    )
    gain_contribution = jnp.sum(normalized_gradient * standardized_rows, axis=0)
    scaled_rows = normalized_gradient * layer_norm_gain
    branch_gradient = inverse_deviation * (
        scaled_rows
        - jnp.mean(scaled_rows, axis=-1, keepdims=True)
        - standardized_rows * jnp.mean(scaled_rows * standardized_rows, axis=-1, keepdims=True)
    )
    return (branch_gradient.astype(jnp.bfloat16), gain_contribution, table_part)


def on_device(
    pixels,
    cotangent,
    embed_weight,
    embed_bias,
    layer_norm_gain,
    qkv_weight,
    out_weight,
    bias_table,
    rel_index,
    shifts,
):
    images, rows_dev, cols_dev, features = cotangent.shape
    head_count = bias_table.shape[0]
    grid_rows = rows_dev * lax.axis_size("row")
    grid_cols = cols_dev * lax.axis_size("col")
    row_shift = shifts[:, 0]
    col_shift = shifts[:, 1]
    qkv_rowwise = lax.all_gather(qkv_weight, "row", axis=0, tiled=True)
    qkv_full, out_columns = (
        lax.all_gather(qkv_rowwise, ("col", "dp"), axis=1, tiled=True),
        lax.all_gather(out_weight, ("col", "dp"), axis=1, tiled=True),
    )
    patches = make_patches(pixels)
    tokens = embed_cells(patches, embed_weight, embed_bias)
    below = from_behind((tokens, cotangent), "row", -1)
    shifted = splice_after(tokens, below[0], row_shift, 1)
    shifted_cot = splice_after(cotangent, below[1], row_shift, 1)
    beside = from_behind((shifted[:, :, :WIN], shifted_cot[:, :, :WIN]), "col", -1)
    shifted = splice_after(shifted, beside[0], col_shift, 2)
    shifted_cot = splice_after(shifted_cot, beside[1], col_shift, 2)
    row_ids = lax.axis_index("row") * rows_dev + jnp.arange(rows_dev, dtype=jnp.int32)
    col_ids = lax.axis_index("col") * cols_dev + jnp.arange(cols_dev, dtype=jnp.int32)
    row_part = (row_ids[None, :] >= grid_rows - row_shift[:, None]).astype(jnp.int32)
    col_part = (col_ids[None, :] >= grid_cols - col_shift[:, None]).astype(jnp.int32)
    region = 2 * row_part[:, :, None] + col_part[:, None, :]
    labels = window_split(region.reshape(images * rows_dev, cols_dev, 1))[:, :, 0]
    cell_windows = window_split(shifted.reshape(images * rows_dev, cols_dev, features))
    cot_flat = window_split(shifted_cot.reshape(images * rows_dev, cols_dev, features)).reshape(
        -1, features
    )
    selector = (
        rel_index.reshape(-1)[:, None] == jnp.arange(bias_table.shape[1], dtype=jnp.int32)[None, :]
    ).astype(jnp.float32)
    bias_full = jnp.dot(selector, bias_table.T, precision=lax.Precision.HIGHEST).T.reshape(
        head_count, WIN * WIN, WIN * WIN
    )
    stored_residuals, attended = attend_forward(
        cell_windows, labels, layer_norm_gain, qkv_full, bias_full
    )
    d_attended = lax.dot_general(
        cot_flat,
        lax.all_gather(out_columns, "row", axis=0, tiled=True),
        (((1,), (1,)), ((), ())),
        preferred_element_type=jnp.float32,
    ).astype(jnp.bfloat16)
    partial_rows = lax.psum_scatter(
        lax.dot_general(
            attended, cot_flat, (((0,), (0,)), ((), ())), preferred_element_type=jnp.float32
        ),
        "row",
        scatter_dimension=0,
        tiled=True,
    )
    out_weight_grad = lax.psum_scatter(partial_rows, ("col", "dp"), scatter_dimension=1, tiled=True)
    d_rows, gain_contribution, table_part = attend_backward(
        stored_residuals, d_attended, layer_norm_gain, qkv_full
    )
    branch_gradient = window_join(
        d_rows.reshape(-1, WIN * WIN, features), images * rows_dev, cols_dev
    ).reshape(images, rows_dev, cols_dev, features)
    patch_rows = patches.reshape(-1, patches.shape[-1])
    cot_rows = cotangent.reshape(-1, features)
    contract = (((0,), (0,)), ((), ()))
    behind = from_behind(branch_gradient[:, :, cols_dev - WIN :], "col", 1)
    d_back = splice_before(branch_gradient, behind, col_shift, 2)
    above = from_behind(d_back, "row", 1)
    d_back = splice_before(d_back, above, row_shift, 1)
    back_rows = d_back.reshape(-1, features)
    embed_grad = lax.dot_general(
        patch_rows, cot_rows, contract, preferred_element_type=jnp.float32
    ) + lax.dot_general(patch_rows, back_rows, contract, preferred_element_type=jnp.float32)
    bias_grad = jnp.sum(cot_rows, axis=0, dtype=jnp.float32) + jnp.sum(
        back_rows, axis=0, dtype=jnp.float32
    )
    table_grad = jnp.dot(
        table_part.reshape(head_count, -1), selector, precision=lax.Precision.HIGHEST
    )
    totals = lax.psum((embed_grad, bias_grad, gain_contribution, table_grad), ("row", "col", "dp"))
    return (out_weight_grad, totals[0], totals[1], totals[2], totals[3])


def solution(mesh):
    return jax.shard_map(
        on_device,
        mesh=mesh,
        in_specs=(
            P("dp", None, "row", "col"),
            P("dp", "row", "col", None),
            P(),
            P(),
            P(),
            P("row", ("col", "dp")),
            P("row", ("col", "dp")),
            P(),
            P(),
            P("dp", None),
        ),
        out_specs=(P("row", ("col", "dp")), P(), P(), P(), P()),
        check_vma=False,
    )
```

profile of v0, /device:TPU:0, one launch (start us, length us, event | category | flops | bytes accessed | tf_op | source)
XLA Modules:
  0.0 390.5 jit_solution(13253919688802146951)
XLA Ops:
  8.0 45.2 %all-gather.4.cloned.1.call-done = bf16[1024,576]{0,1:T(8,128)(2,1)} async-done(((bf16[128,576]{0,1:T(8,128)(2,1)}), bf16[1024,576]{0,1:T(8,128)(2,1)}) %all-gather.4.cloned.1.call-update) | async-done | bytes 1179664 | tf_op jit(solution)/shard_map/all_gather | solution.py:184
  53.2 2.1 collective-permute-start.2
  55.4 2.4 reshape.177
  60.0 12.5 %all_gather.14 = bf16[96,1024]{1,0:T(8,128)(2,1)} all-gather(bf16[96,256]{1,0:T(8,128)(2,1)S(1)} %copy-done.13), channel_id=1, replica_groups=mesh['row'=8,'col'=2,'dp'=2] {'col','dp'}, dimensions={1}, use_global_device_ids=true | all-gather | bytes 245760 | tf_op jit(solution)/shard_map/all_gather | solution.py:187
  76.8 2.6 convolution_bitcast_fusion
  86.7 7.0 %all-gather.6.cloned.1.call-done = bf16[1024,2304]{0,1:T(8,128)(2,1)} async-done(((bf16[1024,576]{0,1:T(8,128)(2,1)}), bf16[1024,2304]{0,1:T(8,128)(2,1)}) %all-gather.6.cloned.1.call-update) | async-done | bytes 4718608 | tf_op jit(solution)/shard_map/all_gather | solution.py:186
  93.7 3.8 convolution_convert_fusion
  99.9 2.5 reshape.366
  102.5 1.6 reshape.367
  104.1 1.8 copy.178
  107.3 1.6 fusion.45
  109.0 3.8 fusion.7
  112.7 2.7 copy.168
  115.4 2.5 reshape.182
  117.9 3.4 fusion.46
  121.5 17.9 %all-gather.8.cloned.1.call-done = bf16[768,1024]{1,0:T(8,128)(2,1)} async-done(((bf16[96,1024]{1,0:T(8,128)(2,1)}), bf16[768,1024]{1,0:T(8,128)(2,1)}) %all-gather.8.cloned.1.call-update) | async-done | bytes 1572880 | tf_op jit(solution)/shard_map/all_gather | solution.py:218
  139.4 3.0 convolution_convert_fusion.3
  142.4 2.4 reshape.369
  144.8 2.5 copy.182
  147.3 2.8 multiply_reduce_fusion
  153.8 2.3 copy.177
  156.0 2.5 reshape.185
  160.0 1.6 copy.181
  162.8 3.5 fusion.8
  166.3 1.8 copy.184
  169.3 4.2 %multiply_reduce_fusion.1 = (f32[1024]{0:T(1024)S(1)}, f32[256]{0:T(256)S(1)}, f32[256]{0:T(256)S(1)}, f32[256,1024]{1,0:T(8,128)S(1)}) fusion(f32[1,4,8,8,1024]{4,3,2,1,0:T(8,128)S(1)} %copy.156, f32[256]{0:T(256)S(1)} %rsqrt.12, f32[256]{0:T(256)S(1)} %div.23, f32[1024]{0:T(1024)S(1)} %copy-done.15, bf16[1024,2304]{0,1:T(8,128)(2,1)} %all-gather.6.cloned.1.call-done, ...), kind=kOutput, calls=%fused_computation.41 | convolution fusion | flops 1213594112 | bytes 8007680 | tf_op jit(solution)/shard_map/dot_general | solution.py:153
  177.6 15.2 %collective-permute-done.5 = bf16[1,8,32,1024]{3,2,1,0:T(8,128)(2,1)S(1)} collective-permute-done((bf16[1,8,32,1024]{3,2,1,0:T(8,128)(2,1)S(1)}, bf16[1,8,32,1024]{3,2,1,0:T(8,128)(2,1)S(1)}, u32[]{:S(2)}, u32[]{:S(2)}) %collective-permute-start.5) | collective-permute-done | bytes 524320 | tf_op jit(solution)/shard_map/ppermute | solution.py:14
  194.0 33.6 %reduce-scatter.3.cloned.1.call-done = f32[96,1024]{1,0:T(8,128)} async-done(((f32[768,1024]{1,0:T(8,128)}), f32[96,1024]{1,0:T(8,128)}) %reduce-scatter.3.cloned.1.call-update) | async-done | bytes 393232 | tf_op jit(solution)/shard_map/reduce_scatter | solution.py:222
  229.5 40.2 %all-reduce.2 = (f32[1024]{0:T(1024)}, f32[1024]{0:T(1024)}, f32[12,225]{1,0:T(8,128)}) all-reduce(f32[1024]{0:T(1024)S(1)} %add.134, f32[1024]{0:T(1024)S(1)} %get-tuple-element.71, f32[12,225]{1,0:T(8,128)S(1)} %fusion.1), channel_id=1, replica_groups=mesh['row'=8,'col'=2,'dp'=2] {'row','col','dp'}, use_global_device_ids=true, to_apply=%region_12.13 | all-reduce | flops 4748 | bytes 37984 | tf_op jit(solution)/shard_map/psum | solution.py:254
  269.7 87.6 %all-reduce.5.cloned.1.call-done = f32[48,1024]{1,0:T(8,128)} async-done(((f32[48,1024]{1,0:T(8,128)}), f32[48,1024]{1,0:T(8,128)}) %all-reduce.5.cloned.1.call-update) | async-done | bytes 196624 | tf_op jit(solution)/shard_map/psum | solution.py:254
  357.4 24.7 %reduce-scatter.5.cloned.1.call-done = f32[96,256]{1,0:T(8,128)} async-done(((f32[96,1024]{1,0:T(8,128)}), f32[96,256]{1,0:T(8,128)}) %reduce-scatter.5.cloned.1.call-update) | async-done | bytes 98320 | tf_op jit(solution)/shard_map/reduce_scatter | solution.py:230
  382.1 1.6 copy.218
  (113 shorter events, 25.2 us)
Async XLA Ops:
  7.2 51.3 %copy-start = (bf16[48,1024]{1,0:T(8,128)(2,1)S(1)}, bf16[48,1024]{1,0:T(8,128)(2,1)}, u32[]{:S(2)}) copy-start(bf16[48,1024]{1,0:T(8,128)(2,1)} %param.12) | copy-start | bytes 294916
  7.2 51.3 %copy-start.18 = (f32[1024]{0:T(1024)S(1)}, f32[1024]{0:T(1024)}, u32[]{:S(2)}) copy-start(f32[1024]{0:T(1024)} %param.13) | copy-start | bytes 12292
  7.2 45.9 %all-gather.4.cloned.1.call-start = ((), (), s32[]{:S(2)}) async-start(), calls=%async_computation.2 | async-start | bytes 1327104 | tf_op jit(solution)/shard_map/all_gather | solution.py:184
  7.9 85.8 %all-gather.6.cloned.1.call-start = ((), (), s32[]{:S(2)}) async-start(), calls=%async_computation.3 | async-start | bytes 5898240 | tf_op jit(solution)/shard_map/all_gather | solution.py:186
  53.1 6.9 %copy-start.13 = (bf16[96,256]{1,0:T(8,128)(2,1)S(1)}, bf16[96,256]{1,0:T(8,128)(2,1)}, u32[]{:S(2)}) copy-start(bf16[96,256]{1,0:T(8,128)(2,1)} %param.16) | copy-start | bytes 147460
  53.2 19.5 %copy-start.19 = (s32[1,2]{1,0:T(1,128)S(1)}, s32[1,2]{1,0:T(1,128)}, u32[]{:S(2)}) copy-start(s32[1,2]{1,0:T(1,128)} %param.19) | copy-start | bytes 28
  53.2 22.8 %copy-start.14 = (s32[64,64]{1,0:T(8,128)S(1)}, s32[64,64]{1,0:T(8,128)}, u32[]{:S(2)}) copy-start(s32[64,64]{1,0:T(8,128)} %param.18) | copy-start | bytes 49156
  53.2 23.6 %copy-start.20 = (f32[12,225]{1,0:T(8,128)S(1)}, f32[12,225]{1,0:T(8,128)}, u32[]{:S(2)}) copy-start(f32[12,225]{1,0:T(8,128)} %param.17) | copy-start | bytes 32404
  53.2 86.2 %all-gather.8.cloned.1.call-start = ((), (), s32[]{:S(2)}) async-start(), calls=%async_computation.6 | async-start | bytes 1769472 | tf_op jit(solution)/shard_map/all_gather | solution.py:218
  53.2 29.6 %collective-permute-start.2 = (bf16[1,8,32,1024]{3,2,1,0:T(8,128)(2,1)}, bf16[1,8,32,1024]{3,2,1,0:T(8,128)(2,1)S(1)}, u32[]{:S(2)}, u32[]{:S(2)}) collective-permute-start(bf16[1,8,32,1024]{3,2,1,0:T(8,128)(2,1)} %param.11), channel_id=1, source_target_pairs={{0,28},{4,0},{8,4},{12,8},{16,12},{20,16},{24,20},{28,24},{1,29},{... | collective-permute-start | bytes 1572872 | tf_op jit(solution)/shard_map/ppermute | solution.py:14
  58.5 20.9 %copy-start.8 = (bf16[1,8,32,3,4,4]{2,1,5,4,3,0:T(8,128)(2,1)}, bf16[1,8,32,3,4,4]{2,1,5,4,3,0:T(8,128)(2,1)S(1)}, u32[]{:S(2)}) copy-start(bf16[1,8,32,3,4,4]{2,1,5,4,3,0:T(8,128)(2,1)S(1)} %copy.154) | copy-start | bytes 73732
  58.8 20.5 %collective-permute-start = (bf16[1,8,32,1024]{3,2,1,0:T(8,128)(2,1)S(1)}, bf16[1,8,32,1024]{3,2,1,0:T(8,128)(2,1)S(1)}, u32[]{:S(2)}, u32[]{:S(2)}) collective-permute-start(bf16[1,8,32,1024]{3,2,1,0:T(8,128)(2,1)S(1)} %fusion.11), channel_id=1, source_target_pairs={{0,28},{4,0},{8,4},{12,8},{16,12},{20,16},{24,20},{28,24},{1,29},{... | collective-permute-start | bytes 1572872 | tf_op jit(solution)/shard_map/ppermute | solution.py:14
  72.6 155.0 %reduce-scatter.3.cloned.1.call-start = ((), (), s32[]{:S(2)}) async-start(), calls=%async_computation.4 | async-start | bytes 3538944 | tf_op jit(solution)/shard_map/reduce_scatter | solution.py:222
  76.1 3.3 copy-start.16
  79.4 3.5 copy-start.5
  79.6 4.0 %collective-permute-start.1 = (bf16[1,8,8,1024]{3,2,1,0:T(8,128)(2,1)S(1)}, bf16[1,8,8,1024]{3,2,1,0:T(8,128)(2,1)S(1)}, u32[]{:S(2)}, u32[]{:S(2)}) collective-permute-start(bf16[1,8,8,1024]{3,2,1,0:T(8,128)(2,1)S(1)} %slice.150), channel_id=1, source_target_pairs={{0,2},{2,0},{1,3},{3,1},{4,6},{6,4},{5,7},{7,5},{8,10},{10,8},{9,1... | collective-permute-start | bytes 393224 | tf_op jit(solution)/shard_map/ppermute | solution.py:14
  83.1 1.5 collective-permute-start.3
  99.9 2.6 copy-start.7
  107.3 1.6 copy-start.3
  121.3 236.1 %all-reduce.5.cloned.1.call-start = ((), (), s32[]{:S(2)}) async-start(), calls=%async_computation.7 | async-start | bytes 393216 | tf_op jit(solution)/shard_map/psum | solution.py:254
  147.3 2.8 copy-start.4
  151.4 0.9 copy-start.1
  153.8 4.8 %copy-start.2 = (bf16[4,12,64,64]{2,3,1,0:T(8,128)(2,1)S(1)}, bf16[4,12,64,64]{2,3,1,0:T(8,128)(2,1)}, u32[]{:S(2)}) copy-start(bf16[4,12,64,64]{2,3,1,0:T(8,128)(2,1)} %copy-done.1) | copy-start | bytes 1179652
  160.0 2.9 copy-start.10
  166.3 3.1 copy-start.11
  166.3 3.1 copy-start.12
  173.9 2.7 copy-start.9
  174.0 1.4 collective-permute-start.4
  175.6 17.2 %collective-permute-start.5 = (bf16[1,8,32,1024]{3,2,1,0:T(8,128)(2,1)S(1)}, bf16[1,8,32,1024]{3,2,1,0:T(8,128)(2,1)S(1)}, u32[]{:S(2)}, u32[]{:S(2)}) collective-permute-start(bf16[1,8,32,1024]{3,2,1,0:T(8,128)(2,1)S(1)} %fusion.25), channel_id=1, source_target_pairs={{0,4},{4,8},{8,12},{12,16},{16,20},{20,24},{24,28},{28,0},{1,5},{5... | collective-permute-start | bytes 1572872 | tf_op jit(solution)/shard_map/ppermute | solution.py:14
  192.7 35.0 %copy-start.6 = (f32[12,64,64]{1,2,0:T(8,128)S(1)}, f32[12,64,64]{1,2,0:T(8,128)}, u32[]{:S(2)}) copy-start(f32[12,64,64]{1,2,0:T(8,128)} %get-tuple-element.81) | copy-start | bytes 589828
  193.0 35.0 %copy-start.17 = (s32[4096]{0:T(1024)S(1)}, s32[4096]{0:T(1024)}, u32[]{:S(2)}) copy-start(s32[4096]{0:T(1024)} %copy-done.16) | copy-start | bytes 49156
  193.9 188.1 %reduce-scatter.5.cloned.1.call-start = ((), (), s32[]{:S(2)}) async-start(), calls=%async_computation.5 | async-start | bytes 491520 | tf_op jit(solution)/shard_map/reduce_scatter | solution.py:230
  (1 other events, 0.7 us)
Sparse Core Ops, SparseCore 0:
  10.0 43.0 all-gather.3
  54.7 38.9 all-gather.5
  95.9 43.4 all-gather.7
  142.9 84.6 reduce-scatter.2
  233.6 123.7 all-reduce.4
  360.3 21.7 reduce-scatter.4
where the time goes:
time: 391 us
  waiting for transfers between devices  233 us (60%)
  blocking collectives  52.7 us (13%)
  local copies, waits for them, and re-layouts  38.4 us (10%)
  matrix products  34.1 us (9%)
  between operations  22.4 us (6%)
  other arithmetic  5.59 us (1%)
  starting transfers between devices  4.81 us (1%)
    psum x1, waiting for transfers between devices, on_device(): lax.psum((embed_grad, bias_grad, gain_contribution, table_grad), ('row',...  87.6 us
    all_gather x1, waiting for transfers between devices, on_device(): qkv_rowwise = lax.all_gather(qkv_weight, 'row', axis=0, tiled=True)  45.2 us
    psum x1, blocking collectives, on_device(): lax.psum((embed_grad, bias_grad, gain_contribution, table_grad), ('row',...  40.2 us
    reduce_scatter x1, waiting for transfers between devices, on_device(): lax.psum_scatter(lax.dot_general(attended, cot_flat, (((0,), (0,)), ((),...  33.6 us
    reduce_scatter x1, waiting for transfers between devices, on_device(): lax.psum_scatter(partial_rows, ('col', 'dp'), scatter_dimension=1, tiled=...  24.7 us
    all_gather x1, waiting for transfers between devices, on_device(): lax.all_gather(out_columns, 'row', axis=0, tiled=True)  17.9 us
    ppermute x6, waiting for transfers between devices, from_behind(): return lax.ppermute(value, axis, pairs)  15.7 us
    all_gather x1, blocking collectives, on_device(): lax.all_gather(out_weight, ('col', 'dp'), axis=1, tiled=True)  12.5 us
  transfers between devices with their start and end apart: 12, of which 8 were waited for; matrix products, arithmetic and copies ran while one was open for 19% of the time, Pallas kernels for 0%

commit v1 on v0

--- a/solution.py
+++ b/solution.py
@@ -251,7 +251,9 @@
     table_grad = jnp.dot(
         table_part.reshape(head_count, -1), selector, precision=lax.Precision.HIGHEST
     )
-    totals = lax.psum((embed_grad, bias_grad, gain_contribution, table_grad), ("row", "col", "dp"))
+    totals = lax.psum(
+        lax.psum((embed_grad, bias_grad, gain_contribution, table_grad), ("col", "dp")), "row"
+    )
     return (out_weight_grad, totals[0], totals[1], totals[2], totals[3])
 
 

time: 391 us -> 414 us (1.059)
  waiting for transfers between devices: 233 us -> 257 us
  local copies, waits for them, and re-layouts: 38.4 us -> 26.7 us
  blocking collectives: 52.7 us -> 62.2 us
    reduce_scatter x1, waiting for transfers between devices: 33.6 us -> 77.7 us  [on_device(): lax.psum_scatter(lax.dot_general(attended, cot_flat, (((0,), (0,)), ((),...]
    psum x1 -> x2, waiting for transfers between devices: 87.6 us -> 49.4 us  [the longest x1 27.1 us: on_device(): lax.psum((embed_grad, bias_grad, gain_contribution, table_grad), ('col',...]
    all_gather x1, waiting for transfers between devices: 7.04 us -> 31.3 us  [on_device(): lax.all_gather(qkv_rowwise, ('col', 'dp'), axis=1, tiled=True)]
    all_gather x1, waiting for transfers between devices: 45.2 us -> 31.7 us  [on_device(): qkv_rowwise = lax.all_gather(qkv_weight, 'row', axis=0, tiled=True)]
    ppermute x6, waiting for transfers between devices: 15.7 us -> 25.1 us  [from_behind(): return lax.ppermute(value, axis, pairs)]
    psum x1 -> x2, blocking collectives: 40.2 us -> 48.8 us  [the longest x1 36 us: on_device(): lax.psum(lax.psum((embed_grad, bias_grad, gain_contribution, table_grad),...]
  transfers between devices with their start and end apart: 12 -> 13, of which waited for: 8 -> 10; matrix products, arithmetic and copies ran while one was open for 19% -> 6% of each run, Pallas kernels for 0% -> 0%
where the time goes in v1:
time: 414 us
  waiting for transfers between devices  257 us (62%)
  blocking collectives  62.2 us (15%)
  matrix products  32.4 us (8%)
  local copies, waits for them, and re-layouts  26.7 us (6%)
  between operations  22.4 us (5%)
  other arithmetic  7.36 us (2%)
  starting transfers between devices  6.07 us (1%)
    reduce_scatter x1, waiting for transfers between devices, on_device(): lax.psum_scatter(lax.dot_general(attended, cot_flat, (((0,), (0,)), ((),...  77.7 us
    psum x1, blocking collectives, on_device(): lax.psum(lax.psum((embed_grad, bias_grad, gain_contribution, table_grad),...  36 us
    all_gather x1, waiting for transfers between devices, on_device(): qkv_rowwise = lax.all_gather(qkv_weight, 'row', axis=0, tiled=True)  31.7 us
    all_gather x1, waiting for transfers between devices, on_device(): lax.all_gather(qkv_rowwise, ('col', 'dp'), axis=1, tiled=True)  31.3 us
    psum x1, waiting for transfers between devices, on_device(): lax.psum((embed_grad, bias_grad, gain_contribution, table_grad), ('col',...  27.1 us
    ppermute x6, waiting for transfers between devices, from_behind(): return lax.ppermute(value, axis, pairs)  25.1 us
    reduce_scatter x1, waiting for transfers between devices, on_device(): lax.psum_scatter(partial_rows, ('col', 'dp'), scatter_dimension=1, tiled=...  23 us
    psum x1, waiting for transfers between devices, on_device(): lax.psum(lax.psum((embed_grad, bias_grad, gain_contribution, table_grad),...  22.3 us
  transfers between devices with their start and end apart: 13, of which 10 were waited for; matrix products, arithmetic and copies ran while one was open for 6% of the time, Pallas kernels for 0%

profile of v1, /device:TPU:0, one launch (start us, length us, event | category | flops | bytes accessed | tf_op | source)
XLA Modules:
  0.0 413.8 jit_solution(13650641040560871555)
XLA Ops:
  8.0 13.4 %all_gather.14 = bf16[96,1024]{1,0:T(8,128)(2,1)} all-gather(bf16[96,256]{1,0:T(8,128)(2,1)} %param.16), channel_id=1, replica_groups=mesh['row'=8,'col'=2,'dp'=2] {'col','dp'}, dimensions={1}, use_global_device_ids=true | all-gather | bytes 245760 | tf_op jit(solution)/shard_map/all_gather | solution.py:187
  21.5 31.7 %all-gather.4.cloned.1.call-done = bf16[1024,576]{0,1:T(8,128)(2,1)} async-done(((bf16[128,576]{0,1:T(8,128)(2,1)}), bf16[1024,576]{0,1:T(8,128)(2,1)}) %all-gather.4.cloned.1.call-update) | async-done | bytes 1179664 | tf_op jit(solution)/shard_map/all_gather | solution.py:184
  53.2 2.1 collective-permute-start.2
  55.4 1.7 reshape.177
  63.4 2.6 convolution_bitcast_fusion
  66.0 16.5 %collective-permute-done = bf16[1,8,32,1024]{3,2,1,0:T(8,128)(2,1)S(1)} collective-permute-done((bf16[1,8,32,1024]{3,2,1,0:T(8,128)(2,1)S(1)}, bf16[1,8,32,1024]{3,2,1,0:T(8,128)(2,1)S(1)}, u32[]{:S(2)}, u32[]{:S(2)}) %collective-permute-start) | collective-permute-done | bytes 524320 | tf_op jit(solution)/shard_map/ppermute | solution.py:14
  89.8 17.7 %all-gather.8.cloned.1.call-done = bf16[768,1024]{1,0:T(8,128)(2,1)} async-done(((bf16[96,1024]{1,0:T(8,128)(2,1)}), bf16[768,1024]{1,0:T(8,128)(2,1)}) %all-gather.8.cloned.1.call-update) | async-done | bytes 1572880 | tf_op jit(solution)/shard_map/all_gather | solution.py:218
  107.5 2.8 convolution_convert_fusion.3
  110.2 1.7 reshape.369
  112.0 1.6 copy.182
  113.5 31.3 %all-gather.6.cloned.1.call-done = bf16[1024,2304]{0,1:T(8,128)(2,1)} async-done(((bf16[1024,576]{0,1:T(8,128)(2,1)}), bf16[1024,2304]{0,1:T(8,128)(2,1)}) %all-gather.6.cloned.1.call-update) | async-done | bytes 4718608 | tf_op jit(solution)/shard_map/all_gather | solution.py:186
  144.9 3.8 convolution_convert_fusion
  151.1 2.6 reshape.366
  153.7 1.6 reshape.367
  155.3 1.8 copy.178
  158.6 1.7 fusion.45
  160.2 3.6 fusion.8
  163.8 2.6 multiply_reduce_fusion
  170.6 1.8 copy.177
  176.5 4.2 %multiply_reduce_fusion.1 = (f32[1024]{0:T(1024)S(1)}, f32[256]{0:T(256)S(1)}, f32[256]{0:T(256)S(1)}, f32[256,1024]{1,0:T(8,128)S(1)}) fusion(f32[1,4,8,8,1024]{4,3,2,1,0:T(8,128)S(1)} %copy.156, f32[256]{0:T(256)S(1)} %rsqrt.12, f32[256]{0:T(256)S(1)} %div.23, f32[1024]{0:T(1024)S(1)} %copy-done.16, bf16[1024,2304]{0,1:T(8,128)(2,1)} %all-gather.6.cloned.1.call-done, ...), kind=kOutput, calls=%fused_computation.41 | convolution fusion | flops 1213594112 | bytes 8007680 | tf_op jit(solution)/shard_map/dot_general | solution.py:153
  183.0 1.5 collective-permute-start.5
  186.2 3.5 fusion.7
  189.7 1.8 copy.168
  191.9 8.1 %collective-permute-done.5 = bf16[1,8,32,1024]{3,2,1,0:T(8,128)(2,1)} collective-permute-done((bf16[1,8,32,1024]{3,2,1,0:T(8,128)(2,1)S(1)}, bf16[1,8,32,1024]{3,2,1,0:T(8,128)(2,1)}, u32[]{:S(2)}, u32[]{:S(2)}) %collective-permute-start.5) | collective-permute-done | bytes 524320 | tf_op jit(solution)/shard_map/ppermute | solution.py:14
  202.2 2.2 fusion.46
  204.5 27.1 %all-reduce.7.cloned.1.call-done = f32[48,1024]{1,0:T(8,128)} async-done(((f32[48,1024]{1,0:T(8,128)}), f32[48,1024]{1,0:T(8,128)}) %all-reduce.7.cloned.1.call-update) | async-done | bytes 196624 | tf_op jit(solution)/shard_map/psum | solution.py:255
  231.7 77.7 %reduce-scatter.3.cloned.1.call-done = f32[96,1024]{1,0:T(8,128)} async-done(((f32[768,1024]{1,0:T(8,128)}), f32[96,1024]{1,0:T(8,128)}) %reduce-scatter.3.cloned.1.call-update) | async-done | bytes 393232 | tf_op jit(solution)/shard_map/reduce_scatter | solution.py:222
  311.3 12.8 %all-reduce.3 = (f32[1024]{0:T(1024)S(1)}, f32[1024]{0:T(1024)S(1)}, f32[12,225]{1,0:T(8,128)S(1)}) all-reduce(f32[1024]{0:T(1024)S(1)} %add.142, f32[1024]{0:T(1024)S(1)} %get-tuple-element.71, f32[12,225]{1,0:T(8,128)S(1)} %fusion.1), channel_id=1, replica_groups=mesh['row'=8,'col'=2,'dp'=2] {'col','dp'}, use_global_device_ids=true, to_apply=%region_13.14 | all-reduce | flops 4748 | bytes 37984 | tf_op jit(solution)/shard_map/psum | solution.py:255
  324.0 36.0 %all-reduce.2 = (f32[1024]{0:T(1024)}, f32[1024]{0:T(1024)}, f32[12,225]{1,0:T(8,128)}) all-reduce(f32[1024]{0:T(1024)S(1)} %get-tuple-element.77, f32[1024]{0:T(1024)S(1)} %get-tuple-element.78, f32[12,225]{1,0:T(8,128)S(1)} %get-tuple-element.79), channel_id=1, replica_groups=mesh['row'=8,'col'=2,'dp'=2] {'row'}, use_global_device_ids=true, to_apply=%region_14.15 | all-reduce | flops 4748 | bytes 37984 | tf_op jit(solution)/shard_map/psum | solution.py:254
  360.0 22.3 %all-reduce.9.cloned.1.call-done = f32[48,1024]{1,0:T(8,128)} async-done(((f32[48,1024]{1,0:T(8,128)}), f32[48,1024]{1,0:T(8,128)}) %all-reduce.9.cloned.1.call-update) | async-done | bytes 196624 | tf_op jit(solution)/shard_map/psum | solution.py:254
  382.3 23.0 %reduce-scatter.5.cloned.1.call-done = f32[96,256]{1,0:T(8,128)} async-done(((f32[96,1024]{1,0:T(8,128)}), f32[96,256]{1,0:T(8,128)}) %reduce-scatter.5.cloned.1.call-update) | async-done | bytes 98320 | tf_op jit(solution)/shard_map/reduce_scatter | solution.py:230
  405.3 1.6 copy.219
  (119 shorter events, 27.2 us)
Async XLA Ops:
  7.2 50.6 %copy-start = (bf16[48,1024]{1,0:T(8,128)(2,1)S(1)}, bf16[48,1024]{1,0:T(8,128)(2,1)}, u32[]{:S(2)}) copy-start(bf16[48,1024]{1,0:T(8,128)(2,1)} %param.12) | copy-start | bytes 294916
  7.2 46.0 %copy-start.3 = (bf16[1,8,32,1024]{3,2,1,0:T(8,128)(2,1)S(1)}, bf16[1,8,32,1024]{3,2,1,0:T(8,128)(2,1)}, u32[]{:S(2)}) copy-start(bf16[1,8,32,1024]{3,2,1,0:T(8,128)(2,1)} %param.11) | copy-start | bytes 1572868
  7.2 48.2 %copy-start.15 = (bf16[1,3,32,128]{3,2,1,0:T(8,128)(2,1)S(1)}, bf16[1,3,32,128]{3,2,1,0:T(8,128)(2,1)}, u32[]{:S(2)}) copy-start(bf16[1,3,32,128]{3,2,1,0:T(8,128)(2,1)} %param.10) | copy-start | bytes 73732
  7.2 45.9 %all-gather.4.cloned.1.call-start = ((), (), s32[]{:S(2)}) async-start(), calls=%async_computation.2 | async-start | bytes 1327104 | tf_op jit(solution)/shard_map/all_gather | solution.py:184
  7.9 99.5 %all-gather.8.cloned.1.call-start = ((), (), s32[]{:S(2)}) async-start(), calls=%async_computation.6 | async-start | bytes 1769472 | tf_op jit(solution)/shard_map/all_gather | solution.py:218
  21.4 36.4 %copy-start.19 = (f32[1024]{0:T(1024)S(1)}, f32[1024]{0:T(1024)}, u32[]{:S(2)}) copy-start(f32[1024]{0:T(1024)} %param.13) | copy-start | bytes 12292
  21.4 123.4 %all-gather.6.cloned.1.call-start = ((), (), s32[]{:S(2)}) async-start(), calls=%async_computation.3 | async-start | bytes 5898240 | tf_op jit(solution)/shard_map/all_gather | solution.py:186
  53.1 6.1 %copy-start.20 = (s32[1,2]{1,0:T(1,128)S(1)}, s32[1,2]{1,0:T(1,128)}, u32[]{:S(2)}) copy-start(s32[1,2]{1,0:T(1,128)} %param.19) | copy-start | bytes 28
  53.2 9.5 %copy-start.14 = (s32[64,64]{1,0:T(8,128)S(1)}, s32[64,64]{1,0:T(8,128)}, u32[]{:S(2)}) copy-start(s32[64,64]{1,0:T(8,128)} %param.18) | copy-start | bytes 49156
  53.2 10.2 %copy-start.21 = (f32[12,225]{1,0:T(8,128)S(1)}, f32[12,225]{1,0:T(8,128)}, u32[]{:S(2)}) copy-start(f32[12,225]{1,0:T(8,128)} %param.17) | copy-start | bytes 32404
  53.2 178.4 %all-reduce.7.cloned.1.call-start = ((), (), s32[]{:S(2)}) async-start(), calls=%async_computation.7 | async-start | bytes 393216 | tf_op jit(solution)/shard_map/psum | solution.py:255
  53.2 32.7 %collective-permute-start.2 = (bf16[1,8,32,1024]{3,2,1,0:T(8,128)(2,1)S(1)}, bf16[1,8,32,1024]{3,2,1,0:T(8,128)(2,1)S(1)}, u32[]{:S(2)}, u32[]{:S(2)}) collective-permute-start(bf16[1,8,32,1024]{3,2,1,0:T(8,128)(2,1)S(1)} %copy-done.3), channel_id=1, source_target_pairs={{0,28},{4,0},{8,4},{12,8},{16,12},{20,16},{24,20},{28,24},{1,29},{... | collective-permute-start | bytes 1572872 | tf_op jit(solution)/shard_map/ppermute | solution.py:14
  57.8 24.9 %copy-start.10 = (bf16[1,8,32,3,4,4]{2,1,5,4,3,0:T(8,128)(2,1)}, bf16[1,8,32,3,4,4]{2,1,5,4,3,0:T(8,128)(2,1)S(1)}, u32[]{:S(2)}) copy-start(bf16[1,8,32,3,4,4]{2,1,5,4,3,0:T(8,128)(2,1)S(1)} %copy.154) | copy-start | bytes 73732
  58.1 24.4 %collective-permute-start = (bf16[1,8,32,1024]{3,2,1,0:T(8,128)(2,1)S(1)}, bf16[1,8,32,1024]{3,2,1,0:T(8,128)(2,1)S(1)}, u32[]{:S(2)}, u32[]{:S(2)}) collective-permute-start(bf16[1,8,32,1024]{3,2,1,0:T(8,128)(2,1)S(1)} %fusion.11), channel_id=1, source_target_pairs={{0,28},{4,0},{8,4},{12,8},{16,12},{20,16},{24,20},{28,24},{1,29},{... | collective-permute-start | bytes 1572872 | tf_op jit(solution)/shard_map/ppermute | solution.py:14
  62.7 20.0 %copy-start.17 = (s32[4096]{0:T(1024)}, s32[4096]{0:T(1024)S(1)}, u32[]{:S(2)}) copy-start(s32[4096]{0:T(1024)S(1)} %eq.39) | copy-start | bytes 49156
  82.7 4.0 collective-permute-start.1
  86.2 1.5 collective-permute-start.3
  88.1 19.4 %copy-start.5 = (bf16[1,4,8,8,1024]{4,3,2,1,0:T(8,128)(2,1)}, bf16[1,4,8,8,1024]{4,3,2,1,0:T(8,128)(2,1)S(1)}, u32[]{:S(2)}) copy-start(bf16[1,4,8,8,1024]{4,3,2,1,0:T(8,128)(2,1)S(1)} %copy.169) | copy-start | bytes 1572868
  110.2 34.6 %copy-start.13 = (bf16[256,1024]{1,0:T(8,128)(2,1)S(1)}, bf16[256,1024]{1,0:T(8,128)(2,1)}, u32[]{:S(2)}) copy-start(bf16[256,1024]{1,0:T(8,128)(2,1)} %multiply_convert_fusion.3) | copy-start | bytes 1572868
  151.1 2.6 copy-start.8
  163.8 2.6 copy-start.2
  170.6 3.0 copy-start.4
  181.1 4.1 copy-start.11
  181.1 5.1 %copy-start.9 = (bf16[4,64,12,64]{3,2,1,0:T(8,128)(2,1)S(1)}, bf16[4,64,12,64]{3,2,1,0:T(8,128)(2,1)}, u32[]{:S(2)}) copy-start(bf16[4,64,12,64]{3,2,1,0:T(8,128)(2,1)} %reshape.366) | copy-start | bytes 1179652
  181.2 1.6 collective-permute-start.4
  183.0 17.0 %collective-permute-start.5 = (bf16[1,8,32,1024]{3,2,1,0:T(8,128)(2,1)S(1)}, bf16[1,8,32,1024]{3,2,1,0:T(8,128)(2,1)}, u32[]{:S(2)}, u32[]{:S(2)}) collective-permute-start(bf16[1,8,32,1024]{3,2,1,0:T(8,128)(2,1)S(1)} %fusion.25), channel_id=1, source_target_pairs={{0,4},{4,8},{8,12},{12,16},{16,20},{20,24},{24,28},{28,0},{1,5},{5... | collective-permute-start | bytes 1572872 | tf_op jit(solution)/shard_map/ppermute | solution.py:14
  191.9 10.3 %copy-start.6 = (bf16[1,4,8,8,1024]{4,3,2,1,0:T(8,128)(2,1)S(1)}, bf16[1,4,8,8,1024]{4,3,2,1,0:T(8,128)(2,1)}, u32[]{:S(2)}) copy-start(bf16[1,4,8,8,1024]{4,3,2,1,0:T(8,128)(2,1)} %copy-done.5) | copy-start | bytes 1572868
  202.1 107.2 %reduce-scatter.3.cloned.1.call-start = ((), (), s32[]{:S(2)}) async-start(), calls=%async_computation.4 | async-start | bytes 3538944 | tf_op jit(solution)/shard_map/reduce_scatter | solution.py:222
  204.4 105.1 %copy-start.7 = (f32[12,64,64]{1,2,0:T(8,128)S(1)}, f32[12,64,64]{1,2,0:T(8,128)}, u32[]{:S(2)}) copy-start(f32[12,64,64]{1,2,0:T(8,128)} %get-tuple-element.84) | copy-start | bytes 589828
  204.4 105.4 %copy-start.18 = (s32[4096]{0:T(1024)S(1)}, s32[4096]{0:T(1024)}, u32[]{:S(2)}) copy-start(s32[4096]{0:T(1024)} %copy-done.17) | copy-start | bytes 49156
  204.4 177.9 %all-reduce.9.cloned.1.call-start = ((), (), s32[]{:S(2)}) async-start(), calls=%async_computation.8 | async-start | bytes 393216 | tf_op jit(solution)/shard_map/psum | solution.py:254
  231.6 173.7 %reduce-scatter.5.cloned.1.call-start = ((), (), s32[]{:S(2)}) async-start(), calls=%async_computation.5 | async-start | bytes 491520 | tf_op jit(solution)/shard_map/reduce_scatter | solution.py:230
  (3 other events, 3.6 us)
Sparse Core Ops, SparseCore 0:
  10.1 43.0 all-gather.3
  55.3 52.0 all-gather.7
  109.0 35.7 all-gather.5
  202.2 29.2 all-reduce.6
  235.0 74.3 reduce-scatter.2
  312.5 69.7 all-reduce.8
  385.4 19.8 reduce-scatter.4
